TPU v7x, 32 devices: a whole 2x2x4 slice. The times are simulated.
32 devices in a mesh: seq: 2 (over core), ctx: 16 (over z, y, x).
Axes of the slice: x: 2, y: 2, z: 4, core: 2. Of those that a mesh axis runs over, the one named last changes fastest.
Arguments:
- hidden: bfloat16 [32768, 7168], P(('seq', 'ctx')), may hold values from -6 to 6
- router_weight: bfloat16 [7168, 256], replicated, may hold values from -0.0625 to 0.0625
- expert_index: int32 [32768, 8], P(('seq', 'ctx')), may hold values from 0 to 255, all different within a row
- lengths: int32 [2], P('seq'), may hold values from 8192 to 16384
Outputs:
- router_grad: float32 [7168, 256], P('ctx')
- balance: float32 [2], P('seq')
Inputs may be any that keep to these rules, and one draw needn't show every extreme that they name: A sequence's valid tokens are its first lengths[s] slots, the rest are padding. `expert_index`: each row names 8 different experts.
All inputs are finite; a program needn't handle non-finite values.
Results may differ from a plain program's by a relative error of at most 0.0003.
Values sent between devices are 32-bit elements; how exact they have to be, the bound alone decides.
A program may use at most 128 MiB of HBM per device.

v0:
```python
import functools

import jax
import jax.numpy as jnp
from jax import lax
from jax.experimental import pallas as pl
from jax.experimental.pallas import tpu as pltpu
from jax.sharding import PartitionSpec as P

E = 256
TOPK = 8


loss_scale = 65536.0


def shards(hidden, router_weight, expert_index, lengths):
    tok_rows = hidden.shape[0]
    width = hidden.shape[1]
    length_here = lengths[0]
    tokens_live = length_here.astype(jnp.float32)
    positions = lax.axis_index("ctx") * tok_rows + jnp.arange(tok_rows, dtype=jnp.int32)
    valid_mask = (positions < length_here).astype(jnp.float32)
    expert_ids = jnp.arange(E, dtype=jnp.int32)
    expert_hits = jnp.sum((expert_index[:, :, None] == expert_ids).astype(jnp.float32), axis=1)
    counts_local = jnp.sum(valid_mask[:, None] * expert_hits, axis=0)
    logits = jnp.dot(hidden, router_weight, preferred_element_type=jnp.float32)
    scores = jax.nn.sigmoid(logits)
    row_total = jnp.sum(scores, axis=1, keepdims=True)
    share_of = scores / row_total
    score_local = jnp.sum(valid_mask[:, None] * share_of, axis=0)
    counts_all, score_all = lax.psum((counts_local, score_local), "ctx")
    fraction = E * counts_all / (TOPK * tokens_live)
    mean_score = score_all / tokens_live
    balance = jnp.sum(fraction * mean_score).reshape(1)
    weights = loss_scale * fraction / tokens_live
    weighted = jnp.sum(weights * share_of, axis=1, keepdims=True)
    grad_logits = (weights - weighted) / row_total * scores * (1.0 - scores) * valid_mask[:, None]
    seq_count = lax.axis_size("seq")
    ctx_count = lax.axis_size("ctx")
    block_rows = width // (seq_count * ctx_count)
    reordered = hidden.reshape(tok_rows, ctx_count, seq_count, block_rows)
    reordered = jnp.transpose(reordered, (0, 2, 1, 3)).reshape(tok_rows, width)
    columns = reordered.astype(jnp.float32)
    block_sum = lax.psum_scatter(
        lax.dot_general(
            columns,
            grad_logits,
            (((0,), (0,)), ((), ())),
            precision=lax.Precision.HIGHEST,
            preferred_element_type=jnp.float32,
        ),
        ("seq", "ctx"),
        scatter_dimension=0,
        tiled=True,
    )
    router_grad = lax.all_gather(block_sum, "seq", axis=0, tiled=True)
    return (router_grad, balance)


MESH = pl.DeviceIdType.MESH
F32 = jnp.float32
CHUNKS = 2


def remote(src, dst, send, recv, device):
    return pltpu.make_async_remote_copy(
        src_ref=src, dst_ref=dst, send_sem=send, recv_sem=recv, device_id=device, device_id_type=MESH
    )


def kernel(
    n, hid_ref, w_ref, idx_ref, len_ref, out_ref, bal_ref,
    hid, w, sc, gcat, acc, s, fin, cnt, cnt_all, sco, sco_all,
    ra1, ra2, raz, rbz, rb3, rb4,
    in_sem, cs_s, cs_r, ss_s, ss_r, d_s, d_r, ap_s, ap_r, aq_s, aq_r, az_s, az_r, bz_s, bz_r, bp_s, bp_r, f_s, f_r,
):
    c = lax.axis_index("seq")
    me = lax.axis_index("ctx")
    x, y, z = me % 2, (me // 2) % 2, me // 4
    sp, sq = 1 + c, 2 - c
    p = x + c * (y - x)
    q = y + c * (x - y)
    here = p * sp + q * sq
    p_dev = (c, z * 4 + (1 - p) * sp + q * sq)
    q_dev = (c, z * 4 + p * sp + (1 - q) * sq)
    mate_z, across_z = z + 1 - 2 * (z % 2), 3 - z
    zs = [3 * (1 - z // 2), 2 - z // 2, mate_z, z]
    mate = (c, mate_z * 4 + here)
    across = (c, across_z * 4 + here)
    outer = (z == 0) | (z == 3)
    inner = (z == 1) | (z == 2)
    twin = (1 - c, me)

    tok, width = hid.shape
    rows = tok // CHUNKS
    block = width // n
    half = block // 2
    qb = half * 4 // 14
    qa = half - qb

    w_copy = pltpu.make_async_copy(w_ref, w, in_sem.at[CHUNKS])
    w_copy.start()

    def hid_copy(i):
        span = pl.ds(pl.multiple_of(i * rows, rows), rows)
        return pltpu.make_async_copy(hid_ref.at[span], hid.at[span], in_sem.at[i])

    for i in range(CHUNKS):
        hid_copy(i).start()

    barrier = pltpu.get_barrier_semaphore()

    @pl.loop(1, n)
    def _(d):
        pl.semaphore_signal(barrier, inc=1, device_id=(c, (me + d) % n), device_id_type=MESH)

    pl.semaphore_signal(barrier, inc=1, device_id=twin, device_id_type=MESH)

    length_here = len_ref[0]
    live = jnp.full((1, E), length_here, jnp.int32).astype(F32)

    def valid_of(i):
        at = me * tok + i * rows + lax.broadcasted_iota(jnp.int32, (rows, 1), 0)
        return (at < length_here).astype(F32)

    def count_step(i, total):
        span = pl.ds(pl.multiple_of(i * rows, rows), rows)
        ids = lax.broadcasted_iota(jnp.int32, (E, rows), 0)
        named = idx_ref[:, span]
        hits = jnp.zeros((E, rows), F32)
        for k in range(TOPK):
            hits = hits + (named[k : k + 1, :] == ids).astype(F32)
        at = me * tok + i * rows + lax.broadcasted_iota(jnp.int32, (8, rows), 1)
        valid = (at < length_here).astype(F32).astype(jnp.bfloat16)
        return total + lax.dot_general(
            valid, hits.astype(jnp.bfloat16), (((1,), (1,)), ((), ())), preferred_element_type=F32
        )

    counts = lax.fori_loop(0, CHUNKS, count_step, jnp.zeros((8, E), F32))[:1]
    cnt[...] = counts
    cnt_all[me] = counts
    pl.semaphore_wait(barrier, n)

    def stat_copy(d, src, everyone, send, recv):
        return remote(src, everyone.at[me], send.at[d], recv.at[d], (c, (me + d) % n))

    @pl.loop(1, n)
    def _(d):
        stat_copy(d, cnt, cnt_all, cs_s, cs_r).start()

    w_copy.wait()

    def logit_step(i, total):
        span = pl.ds(pl.multiple_of(i * rows, rows), rows)
        hid_copy(i).wait()
        logits = jnp.dot(hid[span, :], w[...], preferred_element_type=F32)
        scores = jax.nn.sigmoid(logits)
        sc[span, :] = scores
        share = scores / jnp.sum(scores, axis=1, keepdims=True)
        return total + jnp.sum(share * valid_of(i), axis=0, keepdims=True)

    score_local = lax.fori_loop(0, CHUNKS, logit_step, jnp.zeros((1, E), F32))
    sco[...] = score_local
    sco_all[me] = score_local

    @pl.loop(1, n)
    def _(d):
        stat_copy(d, cnt, cnt_all, cs_s, cs_r).wait_recv()

    fraction = E * jnp.sum(cnt_all[...], axis=0) / (TOPK * live)
    weights = loss_scale * fraction / live

    @pl.loop(0, CHUNKS)
    def _(i):
        span = pl.ds(pl.multiple_of(i * rows, rows), rows)
        scores = sc[span, :]
        row_total = jnp.sum(scores, axis=1, keepdims=True)
        weighted = jnp.sum(weights * (scores / row_total), axis=1, keepdims=True)
        grad = (weights - weighted) / row_total * scores * (1.0 - scores) * valid_of(i)
        top = grad.astype(jnp.bfloat16)
        gcat[span, :E] = top
        gcat[span, E:] = (grad - top.astype(F32)).astype(jnp.bfloat16)

    @pl.loop(1, n)
    def _(d):
        stat_copy(d, sco, sco_all, ss_s, ss_r).start()

    def pair_send(k, j):
        pair = pl.ds(zs[k] * 4 + 2 * j, 2)
        return remote(acc.at[1 - c, pair], s.at[pair], d_s.at[2 * k + j], d_r.at[2 * k + j], twin)

    def slab_compute(k):
        @pl.loop(0, 2)
        def _(j):
            b = zs[k] * 4 + 2 * j
            columns = pl.ds(pl.multiple_of(b * block, 2 * block), 2 * block)
            both = lax.dot_general(
                hid[:, columns], gcat[...], (((0,), (0,)), ((), ())), preferred_element_type=F32
            )
            part = both[:, :E] + both[:, E:]
            for u in range(2):
                for h in range(2):
                    acc[h, b + u] = part[u * block + h * half : u * block + (h + 1) * half]
            pair_send(k, j).start()

    def slab_join(k):
        for j in range(2):
            pair_send(k, j).wait_recv()

        @pl.loop(0, 4)
        def _(j):
            s[zs[k] * 4 + j] += acc[c, zs[k] * 4 + j]

    lo, hi = pl.ds(0, qa), pl.ds(qa, qb)

    def a_p(k, t):
        return remote(s.at[zs[k] * 4 + (1 - p) * sp + t * sq, lo], ra1.at[k, t], ap_s.at[2 * k + t], ap_r.at[2 * k + t], p_dev)

    def a_q(k):
        return remote(s.at[zs[k] * 4 + p * sp + (1 - q) * sq, lo], ra2.at[k], aq_s.at[k], aq_r.at[k], q_dev)

    def a_at(k):
        return s.at[zs[k] * 4 + here, lo]

    def b_at(k):
        return s.at[pl.ds(zs[k] * 4, 4), hi]

    def line(at, got, send, recv):
        to = [mate, mate, mate, across, across, mate]
        of = [0, 1, 2, 0, 1, 2]
        return [lambda i=i: remote(at(of[i]), got.at[i], send.at[i], recv.at[i], to[i]) for i in range(6)]

    a_z = line(a_at, raz, az_s, az_r)
    b_z = line(b_at, rbz, bz_s, bz_r)

    def outer_send(copies, k):
        @pl.when(outer)
        def _():
            copies[k]().start()

    def inner_pass(copies, at, got, slot, k, out):
        @pl.when(inner)
        def _():
            copies[slot]().wait_recv()
            at(k)[...] += got[slot]
            copies[out]().start()

    def line_end(copies):
        @pl.when(outer)
        def _():
            copies[5]().wait_recv()

        @pl.when(inner)
        def _():
            copies[2]().wait_recv()
            copies[4]().wait_recv()

    def line_sent(copies):
        @pl.when(outer)
        def _():
            for i in range(3):
                copies[i]().wait_send()

        @pl.when(inner)
        def _():
            for i in range(3, 6):
                copies[i]().wait_send()

    def b_p(t):
        return remote(s.at[z * 4 + (1 - p) * sp + t * sq, hi], rb3.at[t], bp_s.at[t], bp_r.at[t], p_dev)

    b_q = remote(s.at[z * 4 + p * sp + (1 - q) * sq, hi], rb4, bp_s.at[2], bp_r.at[2], q_dev)

    def slab_send(k):
        slab_join(k)
        if k < 3:
            outer_send(b_z, k)
        for t in range(2):
            a_p(k, t).start()

    def a_turn(k):
        for t in range(2):
            a_p(k, t).wait_recv()
            s[zs[k] * 4 + p * sp + t * sq, lo] += ra1[k, t]
        a_q(k).start()

    def a_join(k):
        a_q(k).wait_recv()
        a_at(k)[...] += ra2[k]

    for k in range(4):
        slab_compute(k)
        if k > 0:
            slab_send(k - 1)
    inner_pass(b_z, b_at, rbz, 0, 0, 3)
    slab_send(3)
    a_turn(0)
    inner_pass(b_z, b_at, rbz, 1, 1, 4)
    a_turn(1)
    a_join(0)
    outer_send(a_z, 0)
    inner_pass(b_z, b_at, rbz, 3, 2, 5)
    a_turn(2)
    a_join(1)
    outer_send(a_z, 1)
    inner_pass(a_z, a_at, raz, 0, 0, 3)
    a_turn(3)
    line_end(b_z)

    @pl.when(outer)
    def _():
        b_at(3)[...] += rbz[5]

    @pl.when(inner)
    def _():
        b_at(3)[...] += rbz[2] + rbz[4]

    for t in range(2):
        b_p(t).start()
    a_join(2)
    outer_send(a_z, 2)
    inner_pass(a_z, a_at, raz, 1, 1, 4)
    for t in range(2):
        b_p(t).wait_recv()
        s[z * 4 + p * sp + t * sq, hi] += rb3[t]
    b_q.start()
    inner_pass(a_z, a_at, raz, 3, 2, 5)

    @pl.loop(1, n)
    def _(d):
        stat_copy(d, sco, sco_all, ss_s, ss_r).wait_recv()

    mean_score = jnp.sum(sco_all[...], axis=0) / live
    bal_ref[...] = jnp.broadcast_to(jnp.sum(fraction * mean_score, axis=1, keepdims=True), bal_ref.shape)

    b_q.wait_recv()
    fin[c, hi] = s[z * 4 + here, hi] + rb4[...]
    fin_b = remote(fin.at[c, hi], fin.at[c, hi], f_s.at[1], f_r.at[1], twin)
    fin_b.start()
    a_join(3)
    line_end(a_z)

    @pl.when(outer)
    def _():
        fin[c, lo] = s[z * 4 + here, lo] + raz[5]

    @pl.when(inner)
    def _():
        fin[c, lo] = s[z * 4 + here, lo] + raz[2] + raz[4]

    fin_a = remote(fin.at[c, lo], fin.at[c, lo], f_s.at[0], f_r.at[0], twin)
    fin_a.start()
    fin_b.wait_recv()
    fin_a.wait_recv()
    out_ref[pl.ds(0, half), :] = fin[0]
    out_ref[pl.ds(half, half), :] = fin[1]

    @pl.loop(1, n)
    def _(d):
        stat_copy(d, cnt, cnt_all, cs_s, cs_r).wait_send()
        stat_copy(d, sco, sco_all, ss_s, ss_r).wait_send()

    for k in range(4):
        for j in range(2):
            pair_send(k, j).wait_send()
            a_p(k, j).wait_send()
        a_q(k).wait_send()
    line_sent(a_z)
    line_sent(b_z)
    for t in range(2):
        b_p(t).wait_send()
    b_q.wait_send()
    fin_a.wait_send()
    fin_b.wait_send()


def fused(hidden, router_weight, expert_index, lengths):
    n = lax.axis_size("ctx")
    tok, width = hidden.shape
    block = width // n
    half = block // 2
    qb = half * 4 // 14
    qa = half - qb
    dma = pltpu.SemaphoreType.DMA
    bf16 = jnp.bfloat16
    vm = pltpu.VMEM
    grad, bal = pl.pallas_call(
        functools.partial(kernel, n),
        out_shape=(jax.ShapeDtypeStruct((block, E), F32), jax.ShapeDtypeStruct((1, 128), F32)),
        in_specs=[
            pl.BlockSpec(memory_space=pl.ANY),
            pl.BlockSpec(memory_space=pl.ANY),
            pl.BlockSpec(memory_space=pltpu.VMEM),
            pl.BlockSpec(memory_space=pltpu.SMEM),
        ],
        out_specs=(pl.BlockSpec(memory_space=pltpu.VMEM), pl.BlockSpec(memory_space=pltpu.VMEM)),
        scratch_shapes=[
            vm((tok, width), bf16), vm((width, E), bf16), vm((tok, E), F32), vm((tok, 2 * E), bf16),
            vm((2, n, half, E), F32), vm((n, half, E), F32), vm((2, half, E), F32),
            vm((1, E), F32), vm((n, 1, E), F32), vm((1, E), F32), vm((n, 1, E), F32),
            vm((4, 2, qa, E), F32), vm((4, qa, E), F32), vm((6, qa, E), F32), vm((6, 4, qb, E), F32),
            vm((2, qb, E), F32), vm((qb, E), F32),
            dma((CHUNKS + 1,)), dma((n,)), dma((n,)), dma((n,)), dma((n,)), dma((8,)), dma((8,)),
            dma((8,)), dma((8,)), dma((4,)), dma((4,)), dma((6,)), dma((6,)), dma((6,)), dma((6,)),
            dma((3,)), dma((3,)), dma((2,)), dma((2,)),
        ],
        compiler_params=pltpu.CompilerParams(
            collective_id=0, has_side_effects=True, vmem_limit_bytes=60 * 1024 * 1024
        ),
    )(hidden, router_weight, expert_index.T, lengths)
    return grad, bal[0, :1]


def solution(mesh):
    local = fused if (mesh.shape["seq"], mesh.shape["ctx"]) == (2, 16) else shards
    return jax.shard_map(
        local,
        mesh=mesh,
        in_specs=(P(("seq", "ctx"), None), P(), P(("seq", "ctx"), None), P("seq")),
        out_specs=(P("ctx", None), P("seq")),
        check_vma=False,
    )
```

profile of v0, /device:TPU:0, one launch (start us, length us, event | category | flops | bytes accessed | tf_op | source)
XLA Modules:
  0.0 58.4 jit_solution(11194554726397726826)
XLA Ops:
  1.3 53.4 %shard_map.59 = (f32[448,256]{1,0:T(8,128)}, f32[1,128]{1,0:T(1,128)}) custom-call(bf16[1024,7168]{1,0:T(8,128)(2,1)} %hid_ref.1, bf16[7168,256]{1,0:T(8,128)(2,1)} %w_ref.1, s32[8,1024]{1,0:T(8,128)} %bitcast.3, s32[1]{0:T(128)S(6)} %copy.8.len_ref), custom_call_target="tpu_custom_call" | custom-call | tf_op jit(solution)/shard_map/pallas_call | solution.py:388
  54.7 1.8 %copy.9 = f32[448,256]{1,0:T(8,128)} copy(f32[448,256]{1,0:T(8,128)} %get-tuple-element.8) | data formatting | bytes 917504
where the time goes:
time: 58.7 us; the launch traced here: 58.4 us
  Pallas kernels  53.4 us (91%)
  between operations  3.1 us (5%)
  local copies, waits for them, and re-layouts  1.82 us (3%)
    pallas_call x1, Pallas kernels, fused(): pl.pallas_call(functools.partial(kernel, n), out_shape=(jax.ShapeDtypeStr...  53.4 us
    unnamed x1, local copies, waits for them, and re-layouts  1.82 us

commit v1 on v0

--- a/solution.py
+++ b/solution.py
@@ -70,8 +70,8 @@
 
 
 def kernel(
-    n, hid_ref, w_ref, idx_ref, len_ref, out_ref, bal_ref,
-    hid, w, sc, gcat, acc, s, fin, cnt, cnt_all, sco, sco_all,
+    n, hid_ref, w_ref, idx_hbm, len_ref, out_ref, bal_ref,
+    idx_ref, hid, w, sc, gcat, acc, s, fin, cnt, cnt_all, sco, sco_all,
     ra1, ra2, raz, rbz, rb3, rb4,
     in_sem, cs_s, cs_r, ss_s, ss_r, d_s, d_r, ap_s, ap_r, aq_s, aq_r, az_s, az_r, bz_s, bz_r, bp_s, bp_r, f_s, f_r,
 ):
@@ -99,6 +99,8 @@
     qb = half * 4 // 14
     qa = half - qb
 
+    idx_copy = pltpu.make_async_copy(idx_hbm, idx_ref, in_sem.at[CHUNKS + 1])
+    idx_copy.start()
     w_copy = pltpu.make_async_copy(w_ref, w, in_sem.at[CHUNKS])
     w_copy.start()
 
@@ -137,6 +139,7 @@
             valid, hits.astype(jnp.bfloat16), (((1,), (1,)), ((), ())), preferred_element_type=F32
         )
 
+    idx_copy.wait()
     counts = lax.fori_loop(0, CHUNKS, count_step, jnp.zeros((8, E), F32))[:1]
     cnt[...] = counts
     cnt_all[me] = counts
@@ -387,26 +390,26 @@
     vm = pltpu.VMEM
     grad, bal = pl.pallas_call(
         functools.partial(kernel, n),
-        out_shape=(jax.ShapeDtypeStruct((block, E), F32), jax.ShapeDtypeStruct((1, 128), F32)),
+        out_shape=(pltpu.VMEM((block, E), F32), pltpu.VMEM((1, 128), F32)),
         in_specs=[
-            pl.BlockSpec(memory_space=pl.ANY),
-            pl.BlockSpec(memory_space=pl.ANY),
-            pl.BlockSpec(memory_space=pltpu.VMEM),
+            pl.BlockSpec(memory_space=pltpu.HBM),
+            pl.BlockSpec(memory_space=pltpu.HBM),
+            pl.BlockSpec(memory_space=pltpu.HBM),
             pl.BlockSpec(memory_space=pltpu.SMEM),
         ],
         out_specs=(pl.BlockSpec(memory_space=pltpu.VMEM), pl.BlockSpec(memory_space=pltpu.VMEM)),
         scratch_shapes=[
-            vm((tok, width), bf16), vm((width, E), bf16), vm((tok, E), F32), vm((tok, 2 * E), bf16),
+            vm((TOPK, tok), jnp.int32), vm((tok, width), bf16), vm((width, E), bf16), vm((tok, E), F32), vm((tok, 2 * E), bf16),
             vm((2, n, half, E), F32), vm((n, half, E), F32), vm((2, half, E), F32),
             vm((1, E), F32), vm((n, 1, E), F32), vm((1, E), F32), vm((n, 1, E), F32),
             vm((4, 2, qa, E), F32), vm((4, qa, E), F32), vm((6, qa, E), F32), vm((6, 4, qb, E), F32),
             vm((2, qb, E), F32), vm((qb, E), F32),
-            dma((CHUNKS + 1,)), dma((n,)), dma((n,)), dma((n,)), dma((n,)), dma((8,)), dma((8,)),
+            dma((CHUNKS + 2,)), dma((n,)), dma((n,)), dma((n,)), dma((n,)), dma((8,)), dma((8,)),
             dma((8,)), dma((8,)), dma((4,)), dma((4,)), dma((6,)), dma((6,)), dma((6,)), dma((6,)),
             dma((3,)), dma((3,)), dma((2,)), dma((2,)),
         ],
         compiler_params=pltpu.CompilerParams(
-            collective_id=0, has_side_effects=True, vmem_limit_bytes=60 * 1024 * 1024
+            collective_id=0, has_side_effects=True, vmem_limit_bytes=62914560
         ),
     )(hidden, router_weight, expert_index.T, lengths)
     return grad, bal[0, :1]

time: 58.7 us -> 55.4 us (0.944)
  Pallas kernels: 53.4 us -> 52 us
  local copies, waits for them, and re-layouts: 1.82 us -> 0.77 us
  between operations: 3.1 us -> 2.45 us
    pallas_call x1, Pallas kernels: 53.4 us -> 52 us  [fused(): pl.pallas_call(functools.partial(kernel, n), out_shape=(pltpu.VMEM((block...]
    unnamed x1, local copies, waits for them, and re-layouts: 1.82 us -> 0.77 us
where the time goes in v1:
time: 55.4 us; the launch traced here: 55.2 us
  Pallas kernels  52 us (94%)
  between operations  2.45 us (4%)
  local copies, waits for them, and re-layouts  0.77 us (1%)
    pallas_call x1, Pallas kernels, fused(): pl.pallas_call(functools.partial(kernel, n), out_shape=(pltpu.VMEM((block...  52 us

profile of v1, /device:TPU:0, one launch (start us, length us, event | category | flops | bytes accessed | tf_op | source)
XLA Modules:
  0.0 55.2 jit_solution(7797120987733284684)
XLA Ops:
  1.3 52.0 %shard_map.59 = (f32[448,256]{1,0:T(8,128)S(1)}, f32[1,128]{1,0:T(1,128)S(1)}) custom-call(bf16[1024,7168]{1,0:T(8,128)(2,1)} %hid_ref.1, bf16[7168,256]{1,0:T(8,128)(2,1)} %w_ref.1, s32[8,1024]{1,0:T(8,128)} %bitcast.4, s32[1]{0:T(128)S(6)} %copy.9.len_ref), custom_call_target="tpu_custom_call" | custom-call | tf_op jit(solution)/shard_map/pallas_call | solution.py:391
  53.3 0.8 %copy.8 = f32[448,256]{1,0:T(8,128)} copy(f32[448,256]{1,0:T(8,128)S(1)} %get-tuple-element.6) | data formatting | bytes 917504

commit v2 on v1

v2 whole, which is shorter than its diff:
```python
import functools

import jax
import jax.numpy as jnp
from jax import lax
from jax.experimental import pallas as pl
from jax.experimental.pallas import tpu as pltpu
from jax.sharding import PartitionSpec as P

E = 256
TOPK = 8


loss_scale = 65536.0


def shards(hidden, router_weight, expert_index, lengths):
    tok_rows = hidden.shape[0]
    width = hidden.shape[1]
    length_here = lengths[0]
    tokens_live = length_here.astype(jnp.float32)
    positions = lax.axis_index("ctx") * tok_rows + jnp.arange(tok_rows, dtype=jnp.int32)
    valid_mask = (positions < length_here).astype(jnp.float32)
    expert_ids = jnp.arange(E, dtype=jnp.int32)
    expert_hits = jnp.sum((expert_index[:, :, None] == expert_ids).astype(jnp.float32), axis=1)
    counts_local = jnp.sum(valid_mask[:, None] * expert_hits, axis=0)
    logits = jnp.dot(hidden, router_weight, preferred_element_type=jnp.float32)
    scores = jax.nn.sigmoid(logits)
    row_total = jnp.sum(scores, axis=1, keepdims=True)
    share_of = scores / row_total
    score_local = jnp.sum(valid_mask[:, None] * share_of, axis=0)
    counts_all, score_all = lax.psum((counts_local, score_local), "ctx")
    fraction = E * counts_all / (TOPK * tokens_live)
    mean_score = score_all / tokens_live
    balance = jnp.sum(fraction * mean_score).reshape(1)
    weights = loss_scale * fraction / tokens_live
    weighted = jnp.sum(weights * share_of, axis=1, keepdims=True)
    grad_logits = (weights - weighted) / row_total * scores * (1.0 - scores) * valid_mask[:, None]
    seq_count = lax.axis_size("seq")
    ctx_count = lax.axis_size("ctx")
    block_rows = width // (seq_count * ctx_count)
    reordered = hidden.reshape(tok_rows, ctx_count, seq_count, block_rows)
    reordered = jnp.transpose(reordered, (0, 2, 1, 3)).reshape(tok_rows, width)
    columns = reordered.astype(jnp.float32)
    block_sum = lax.psum_scatter(
        lax.dot_general(
            columns,
            grad_logits,
            (((0,), (0,)), ((), ())),
            precision=lax.Precision.HIGHEST,
            preferred_element_type=jnp.float32,
        ),
        ("seq", "ctx"),
        scatter_dimension=0,
        tiled=True,
    )
    router_grad = lax.all_gather(block_sum, "seq", axis=0, tiled=True)
    return (router_grad, balance)


MESH = pl.DeviceIdType.MESH
F32 = jnp.float32
BF16 = jnp.bfloat16
CHUNKS = 7
PARTS = 2
PLANE = 4
LEVELS = 4


def remote(src, dst, send, recv, device):
    return pltpu.make_async_remote_copy(
        src_ref=src, dst_ref=dst, send_sem=send, recv_sem=recv, device_id=device, device_id_type=MESH
    )


def kernel(
    n, hid_ref, w_ref, idx_ref, len_ref, out_ref, bal_ref,
    idx, hid, w, sh, un, gcat, acc, s, fin,
    cnt, cnt_p, cnt_s, cnt_z, cnt_d, tot, sco, sco_p, sco_s, sco_z,
    ra1, ra2, raz, rbz, rb3,
    up, in_sem, st, d_s, d_r, ap_s, ap_r, aq_s, aq_r, az_s, az_r, bz_s, bz_r, bp_s, bp_r, f_s, f_r,
):
    c = lax.axis_index("seq")
    me = lax.axis_index("ctx")
    x, y, z = me % 2, (me // 2) % 2, me // 4
    sp, sq = 1 + c, 2 - c
    p = x + c * (y - x)
    q = y + c * (x - y)
    here = p * sp + q * sq
    p_dev = (c, z * 4 + (1 - p) * sp + q * sq)
    q_dev = (c, z * 4 + p * sp + (1 - q) * sq)
    mate_z, across_z = z + 1 - 2 * (z % 2), 3 - z
    zs = [3 * (1 - z // 2), 2 - z // 2, mate_z, z]
    mate = (c, mate_z * 4 + here)
    across = (c, across_z * 4 + here)
    outer = (z == 0) | (z == 3)
    inner = (z == 1) | (z == 2)
    twin = (1 - c, me)

    def plane_peer(d):
        return (c, z * 4 + (here + d) % PLANE)

    def line_peer(d):
        return (c, ((z + d) % LEVELS) * 4 + here)

    tok, width = hid.shape
    part_w = width // CHUNKS
    big = tok // PARTS
    block = width // n
    half = block // 2
    qb = half * 3 // 14
    qa = half - qb
    qh = qa // 2

    barrier = pltpu.get_barrier_semaphore()
    for d in range(1, PLANE):
        pl.semaphore_signal(barrier, inc=1, device_id=plane_peer(d), device_id_type=MESH)
    pl.semaphore_signal(barrier, inc=1, device_id=twin, device_id_type=MESH)

    @pl.loop((z + 1) * PLANE, n)
    def _(d):
        pl.semaphore_signal(barrier, inc=1, device_id=(c, d), device_id_type=MESH)

    idx_copy = pltpu.make_async_copy(idx_ref, idx, in_sem.at[2 * CHUNKS])
    idx_copy.start()

    def w_copy(i):
        span = pl.ds(pl.multiple_of(i * part_w, part_w), part_w)
        return pltpu.make_async_copy(w_ref.at[span], w.at[span], in_sem.at[CHUNKS + i])

    def hid_copy(i):
        span = pl.ds(pl.multiple_of(i * part_w, part_w), part_w)
        return pltpu.make_async_copy(hid_ref.at[:, span], hid.at[:, span], in_sem.at[i])

    @pl.loop(0, CHUNKS)
    def _(i):
        w_copy(i).start()
        hid_copy(i).start()

    length_here = len_ref[0]
    live = jnp.full((1, E), length_here, jnp.int32).astype(F32)

    def count_step(i, total):
        span = pl.ds(pl.multiple_of(i * big, big), big)
        ids = lax.broadcasted_iota(jnp.int32, (E, big), 0).astype(BF16)
        named = idx[:, span].astype(F32)
        hits = jnp.zeros((E, big), BF16)
        for k in range(TOPK):
            one = jnp.broadcast_to(named[k : k + 1, :], (E, big)).astype(BF16)
            hits = hits + jnp.where(one == ids, BF16(1), BF16(0))
        at = me * tok + i * big + lax.broadcasted_iota(jnp.int32, (8, big), 1)
        valid = (at < length_here).astype(F32).astype(BF16)
        return total + lax.dot_general(
            valid, hits, (((1,), (1,)), ((), ())), preferred_element_type=F32
        )

    def plane_copy(d, src, everyone, base):
        return remote(src, everyone.at[here], st.at[base], st.at[base + 1], plane_peer(d))

    def line_copy(d, src, everyone, base):
        return remote(src, everyone.at[z], st.at[base + 2], st.at[base + 3], line_peer(d))

    def down_copy(d):
        slot = (z - d // PLANE - 1) * PLANE + here
        return remote(cnt, cnt_d.at[slot], st.at[8], st.at[9], (c, d))

    def up_copy(d):
        return remote(cnt_s, cnt_z.at[z], st.at[2], st.at[3], (c, d * PLANE + here))

    def sent(ref, sem):
        remote(ref, ref, sem, sem, twin).wait_send()

    def came(ref, sem):
        remote(ref, ref, sem, sem, twin).wait_recv()

    def plane_send(value, src, everyone, base):
        src[...] = value
        everyone[here] = value
        for d in range(1, PLANE):
            plane_copy(d, src, everyone, base).start()

    def plane_total(everyone, base):
        came(everyone.at[pl.ds(0, PLANE - 1)], st.at[base + 1])
        return jnp.sum(everyone[...], axis=0)
    idx_copy.wait()
    counts = lax.fori_loop(0, PARTS, count_step, jnp.zeros((8, E), F32))[:1]
    pl.semaphore_wait(barrier, PLANE * (z + 1))

    @pl.loop(0, z)
    def _(d):
        pl.semaphore_signal(up, inc=1, device_id=(c, d * PLANE + here), device_id_type=MESH)
    plane_send(counts, cnt, cnt_p, 0)

    @pl.loop(0, z * PLANE)
    def _(d):
        down_copy(d).start()

    sh[...] = jnp.zeros_like(sh)
    turn = 5 - (x + y + 1) // 2

    def logit_step(i):
        @pl.when(i == turn)
        def _():
            total = plane_total(cnt_p, 0)
            cnt_s[...] = total
            tot[...] = total

            @pl.when(z < LEVELS - 1)
            def _():
                pl.semaphore_wait(up, LEVELS - 1 - z)

            @pl.loop(z + 1, LEVELS)
            def _(d):
                up_copy(d).start()

        span = pl.ds(pl.multiple_of(i * part_w, part_w), part_w)
        w_copy(i).wait()
        hid_copy(i).wait()
        sh[...] += jnp.dot(hid[:, span], w[span, :], preferred_element_type=F32)

    pl.loop(0, CHUNKS)(logit_step)

    def score_step(i, total):
        span = pl.ds(pl.multiple_of(i * big, big), big)
        scores = jax.nn.sigmoid(sh[span, :])
        at = me * tok + i * big + lax.broadcasted_iota(jnp.int32, (big, 1), 0)
        valid = (at < length_here).astype(F32)
        share = scores / jnp.sum(scores, axis=1, keepdims=True)
        live_share = share * valid
        sh[span, :] = share
        un[span, :] = live_share * (1.0 - scores)
        return total + jnp.sum(live_share, axis=0, keepdims=True)

    score_local = lax.fori_loop(0, PARTS, score_step, jnp.zeros((1, E), F32))
    for k in range(LEVELS):
        @pl.when(z == k)
        def _():
            total = tot[...]
            if k < LEVELS - 1:
                far = pl.ds(0, PLANE * (LEVELS - 1 - k))
                came(cnt_d.at[far], st.at[9])
                total = total + jnp.sum(cnt_d[far], axis=0)
            if k > 0:
                near = pl.ds(0, k)
                came(cnt_z.at[near], st.at[3])
                total = total + jnp.sum(cnt_z[near], axis=0)
            tot[...] = total

    fraction = E * tot[...] / (TOPK * live)
    weights = loss_scale * fraction / live

    @pl.loop(0, PARTS)
    def _(i):
        span = pl.ds(pl.multiple_of(i * big, big), big)
        weighted = jnp.sum(weights * sh[span, :], axis=1, keepdims=True)
        grad = (weights - weighted) * un[span, :]
        top = grad.astype(BF16)
        gcat[span, :E] = top
        gcat[span, E:] = (grad - top.astype(F32)).astype(BF16)

    plane_send(score_local, sco, sco_p, 4)

    def level(k):
        return jnp.where(k == 0, zs[0], jnp.where(k == 1, zs[1], jnp.where(k == 2, zs[2], zs[3])))

    def pair_at(k, j):
        row = (1 - y) + j * (2 * y - 1)
        zk = zs[k] if isinstance(k, int) else level(k)
        return zk * 4 + 2 * row

    def pair_send(i):
        pair = pl.ds(pair_at(i // 2, i % 2), 2)
        return remote(acc.at[1 - c, pair], s.at[pair], d_s.at[0], d_r.at[i], twin)

    lo, hi = pl.ds(0, qa), pl.ds(qa, qb)

    def side(o):
        return (1 - q) + o * (2 * q - 1)

    def a_p(k, o):
        zk = zs[k] if isinstance(k, int) else level(k)
        return remote(
            s.at[zk * 4 + (1 - p) * sp + side(o) * sq, lo], ra1.at[k, o], ap_s.at[0], ap_r.at[2 * k + o], p_dev
        )

    def a_q(k):
        return remote(s.at[zs[k] * 4 + p * sp + (1 - q) * sq, lo], ra2.at[k], aq_s.at[0], aq_r.at[k], q_dev)

    def a_at(k, h):
        return s.at[zs[k] * 4 + here, pl.ds(h * qh, qh)]

    def b_at(k, j):
        return s.at[pl.ds(pair_at(k, j), 2), hi]

    TO = [mate, mate, mate, across, across, mate]
    OF = [0, 1, 2, 0, 1, 2]
    AT = [0, 1, 3, 2, 4, 5]

    def a_z(i, h):
        return remote(a_at(OF[i], h), raz.at[h, AT[i]], az_s.at[0], az_r.at[min(2 * AT[i], 6) + h], TO[i])

    def b_z(i, h):
        return remote(b_at(OF[i], h), rbz.at[AT[i], h], bz_s.at[0], bz_r.at[2 * AT[i] + h if AT[i] < 3 else 6], TO[i])

    def b_z_out(k, j):
        pair = pl.ds(pair_at(k, j), 2)
        slot = k + k // 2
        return remote(s.at[pair, hi], rbz.at[slot, j], bz_s.at[0], bz_r.at[jnp.minimum(2 * slot + j, 6)], mate)

    def join(i):
        k, j = i // 2, i % 2
        pair_send(i).wait_recv()
        pair = pl.ds(pair_at(k, j), 2)
        s[pair] += acc[c, pair]

        @pl.when((c == 0) & (k < 3))
        def _():
            a_p(k, j).start()

        @pl.when((c == 1) & (k < 3) & (j == 0))
        def _():
            a_p(k, 0).start()
            a_p(k, 1).start()

        @pl.when(outer & (k < 3))
        def _():
            b_z_out(k, j).start()

    def a_turn(k, o):
        a_p(k, o).wait_recv()
        s[zs[k] * 4 + p * sp + side(o) * sq, lo] += ra1[k, o]
        if o == 0:
            a_q(k).start()

    def a_join(k):
        a_q(k).wait_recv()
        s[zs[k] * 4 + here, lo] += ra2[k]

    def a_out(k):
        @pl.when(outer)
        def _():
            for h in range(2):
                a_z(k, h).start()

    def passing(copies, at, got, slot, k, out, h):
        copies(slot, h).wait_recv()
        at(k, h)[...] += got[h, AT[slot]] if got is raz else got[AT[slot], h]
        copies(out, h).start()

    def b_pass(slot, h):
        k, out = {0: (0, 3), 1: (1, 4), 3: (2, 5)}[slot]

        @pl.when(inner)
        def _():
            passing(b_z, b_at, rbz, slot, k, out, h)

    def a_pass(slot, h):
        k, out = {0: (0, 3), 1: (1, 4), 3: (2, 5)}[slot]

        @pl.when(inner)
        def _():
            passing(a_z, a_at, raz, slot, k, out, h)

    def b_end():
        @pl.when(outer)
        def _():
            came(rbz.at[5], bz_r.at[6])
            for h in range(2):
                b_at(3, h)[...] += rbz[5, h]

        @pl.when(inner)
        def _():
            came(rbz.at[pl.ds(3, 2)], bz_r.at[6])
            for h in range(2):
                b_at(3, h)[...] += rbz[3, h] + rbz[4, h]

    def b_p(o):
        return remote(s.at[z * 4 + (1 - p) * sp + side(o) * sq, hi], rb3.at[o], bp_s.at[0], bp_r.at[o], p_dev)

    b_q = remote(s.at[z * 4 + p * sp + (1 - q) * sq, hi], rb3.at[2], bp_s.at[0], bp_r.at[2], q_dev)

    def b_turn(o):
        b_p(o).wait_recv()
        s[z * 4 + p * sp + side(o) * sq, hi] += rb3[o]
        if o == 0:
            b_q.start()

    def fin_a(h):
        part = fin.at[c, pl.ds(h * qh, qh)]
        return remote(part, part, f_s.at[0], f_r.at[0], twin)

    fin_b = remote(fin.at[c, hi], fin.at[c, hi], f_s.at[0], f_r.at[0], twin)

    def a_end(h):
        part = pl.ds(h * qh, qh)

        @pl.when(outer)
        def _():
            came(raz.at[h, 5], az_r.at[6 + h])
            fin[c, part] = s[z * 4 + here, part] + raz[h, 5]

        @pl.when(inner)
        def _():
            came(raz.at[h, pl.ds(3, 2)], az_r.at[6 + h])
            fin[c, part] = s[z * 4 + here, part] + raz[h, 3] + raz[h, 4]

        fin_a(h).start()

    @pl.loop(0, 8)
    def _(i):
        b = pair_at(i // 2, i % 2)
        columns = pl.ds(pl.multiple_of(b * block, 2 * block), 2 * block)
        both = lax.dot_general(
            hid[:, columns], gcat[...], (((0,), (0,)), ((), ())), preferred_element_type=F32
        )
        part = both[:, :E] + both[:, E:]
        for u in range(2):
            for h in range(2):
                acc[h, b + u] = part[u * block + h * half : u * block + (h + 1) * half]
        pair_send(i).start()

        @pl.when(i > 0)
        def _():
            join(i - 1)

        @pl.when(i == 4)
        def _():
            a_turn(0, 0)

        @pl.when(i == 5)
        def _():
            b_pass(0, 0)

        @pl.when(i == 6)
        def _():
            a_turn(0, 1)
            b_pass(0, 1)

    join(7)
    total = plane_total(sco_p, 4)
    sco_s[...] = total
    sco_z[z] = total
    for d in range(1, LEVELS):
        line_copy(d, sco_s, sco_z, 4).start()
    b_pass(3, 0)
    b_pass(1, 0)
    a_turn(1, 0)
    a_join(0)
    a_out(0)
    b_pass(3, 1)
    b_pass(1, 1)
    a_turn(1, 1)
    b_end()
    for o in range(2):
        b_p(o).start()
    for o in range(2):
        a_p(3, o).start()
    a_pass(0, 0)
    a_turn(2, 0)
    a_join(1)
    a_out(1)
    a_pass(0, 1)
    b_turn(0)
    a_turn(2, 1)
    b_turn(1)
    came(sco_z.at[pl.ds(0, LEVELS - 1)], st.at[7])
    mean_score = jnp.sum(sco_z[...], axis=0) / live
    bal_ref[...] = jnp.broadcast_to(jnp.sum(fraction * mean_score, axis=1, keepdims=True), bal_ref.shape)
    a_pass(1, 0)
    a_pass(1, 1)
    a_turn(3, 0)
    a_join(2)
    a_out(2)
    a_pass(3, 0)
    a_pass(3, 1)
    b_q.wait_recv()
    fin[c, hi] = s[z * 4 + here, hi] + rb3[2]
    fin_b.start()
    a_turn(3, 1)
    a_join(3)
    a_end(0)
    a_end(1)
    came(fin.at[1 - c], f_r.at[0])
    out_ref[pl.ds(0, half), :] = fin[0]
    out_ref[pl.ds(half, half), :] = fin[1]

    near = pl.ds(0, PLANE - 1)
    sent(cnt_p.at[near], st.at[0])
    sent(sco_p.at[near], st.at[4])
    sent(sco_z.at[near], st.at[6])
    for k in range(LEVELS):
        @pl.when(z == k)
        def _():
            if k < LEVELS - 1:
                sent(cnt_z.at[pl.ds(0, LEVELS - 1 - k)], st.at[2])
            if k > 0:
                sent(cnt_d.at[pl.ds(0, PLANE * k)], st.at[8])

    sent(s, d_s.at[0])
    sent(ra1, ap_s.at[0])
    sent(ra2, aq_s.at[0])
    sent(raz.at[0], az_s.at[0])
    sent(rbz.at[pl.ds(0, 3)], bz_s.at[0])
    sent(rb3, bp_s.at[0])
    sent(fin.at[c], f_s.at[0])


def fused(hidden, router_weight, expert_index, lengths):
    n = lax.axis_size("ctx")
    tok, width = hidden.shape
    block = width // n
    half = block // 2
    qb = half * 3 // 14
    qa = half - qb
    dma = pltpu.SemaphoreType.DMA
    vm = pltpu.VMEM
    grad, bal = pl.pallas_call(
        functools.partial(kernel, n),
        out_shape=(pltpu.VMEM((block, E), F32), pltpu.VMEM((1, 128), F32)),
        in_specs=[
            pl.BlockSpec(memory_space=pltpu.HBM),
            pl.BlockSpec(memory_space=pltpu.HBM),
            pl.BlockSpec(memory_space=pltpu.HBM),
            pl.BlockSpec(memory_space=pltpu.SMEM),
        ],
        out_specs=(pl.BlockSpec(memory_space=pltpu.VMEM), pl.BlockSpec(memory_space=pltpu.VMEM)),
        scratch_shapes=[
            vm((TOPK, tok), jnp.int32), vm((tok, width), BF16), vm((width, E), BF16),
            vm((tok, E), F32), vm((tok, E), F32), vm((tok, 2 * E), BF16),
            vm((2, n, half, E), F32), vm((n, half, E), F32), vm((2, half, E), F32),
            vm((1, E), F32), vm((PLANE, 1, E), F32), vm((1, E), F32), vm((LEVELS, 1, E), F32),
            vm((PLANE * (LEVELS - 1), 1, E), F32), vm((1, E), F32),
            vm((1, E), F32), vm((PLANE, 1, E), F32), vm((1, E), F32), vm((LEVELS, 1, E), F32),
            vm((4, 2, qa, E), F32), vm((4, qa, E), F32), vm((2, 6, qa // 2, E), F32), vm((6, 2, 2, qb, E), F32),
            vm((3, qb, E), F32), pltpu.SemaphoreType.REGULAR,
            dma((2 * CHUNKS + 1,)), dma((10,)), dma((1,)), dma((8,)),
            dma((1,)), dma((8,)), dma((1,)), dma((4,)), dma((1,)), dma((8,)), dma((1,)), dma((7,)),
            dma((1,)), dma((3,)), dma((1,)), dma((1,)),
        ],
        compiler_params=pltpu.CompilerParams(
            collective_id=0, has_side_effects=True, vmem_limit_bytes=62914560
        ),
    )(hidden, router_weight, expert_index.T, lengths)
    return grad, bal[0, :1]


def solution(mesh):
    local = fused if (mesh.shape["seq"], mesh.shape["ctx"]) == (2, 16) else shards
    return jax.shard_map(
        local,
        mesh=mesh,
        in_specs=(P(("seq", "ctx"), None), P(), P(("seq", "ctx"), None), P("seq")),
        out_specs=(P("ctx", None), P("seq")),
        check_vma=False,
    )
```

time: 55.4 us -> 47.4 us (0.86)
  Pallas kernels: 52 us -> 44 us
    pallas_call x1, Pallas kernels: 52 us -> 44 us  [fused(): pl.pallas_call(functools.partial(kernel, n), out_shape=(pltpu.VMEM((block...]
where the time goes in v2:
time: 47.4 us; the launch traced here: 47.3 us
  Pallas kernels  44 us (93%)
  between operations  2.45 us (5%)
  local copies, waits for them, and re-layouts  0.77 us (2%)
    pallas_call x1, Pallas kernels, fused(): pl.pallas_call(functools.partial(kernel, n), out_shape=(pltpu.VMEM((block...  44 us

profile of v2, /device:TPU:0, one launch (start us, length us, event | category | flops | bytes accessed | tf_op | source)
XLA Modules:
  0.0 47.3 jit_solution(5085712011668773236)
XLA Ops:
  1.3 44.0 %shard_map.59 = (f32[448,256]{1,0:T(8,128)S(1)}, f32[1,128]{1,0:T(1,128)S(1)}) custom-call(bf16[1024,7168]{1,0:T(8,128)(2,1)} %hid_ref.1, bf16[7168,256]{1,0:T(8,128)(2,1)} %w_ref.1, s32[8,1024]{1,0:T(8,128)} %bitcast.4, s32[1]{0:T(128)S(6)} %copy.9.len_ref), custom_call_target="tpu_custom_call" | custom-call | tf_op jit(solution)/shard_map/pallas_call | solution.py:517
  45.3 0.8 %copy.8 = f32[448,256]{1,0:T(8,128)} copy(f32[448,256]{1,0:T(8,128)S(1)} %get-tuple-element.6) | data formatting | bytes 917504

commit v3 on v2

--- a/solution.py
+++ b/solution.py
@@ -63,6 +63,7 @@
 BF16 = jnp.bfloat16
 CHUNKS = 7
 PARTS = 2
+SMALL = 4
 PLANE = 4
 LEVELS = 4
 
@@ -74,8 +75,8 @@
 
 
 def kernel(
-    n, hid_ref, w_ref, idx_ref, len_ref, out_ref, bal_ref,
-    idx, hid, w, sh, un, gcat, acc, s, fin,
+    n, hid_ref, w_ref, idx_ref, len_hbm, out_ref, bal_ref,
+    len_ref, idx, hid, w, sh, un, gcat, acc, s, fin,
     cnt, cnt_p, cnt_s, cnt_z, cnt_d, tot, sco, sco_p, sco_s, sco_z,
     ra1, ra2, raz, rbz, rb3,
     up, in_sem, st, d_s, d_r, ap_s, ap_r, aq_s, aq_r, az_s, az_r, bz_s, bz_r, bp_s, bp_r, f_s, f_r,
@@ -106,12 +107,32 @@
     tok, width = hid.shape
     part_w = width // CHUNKS
     big = tok // PARTS
+    small = tok // SMALL
     block = width // n
     half = block // 2
     qb = half * 3 // 14
     qa = half - qb
     qh = qa // 2
 
+    len_copy = pltpu.make_async_copy(len_hbm, len_ref, in_sem.at[2 * CHUNKS + 1])
+    len_copy.start()
+    idx_copy = pltpu.make_async_copy(idx_ref, idx, in_sem.at[2 * CHUNKS])
+    idx_copy.start()
+
+    def w_copy(i):
+        span = pl.ds(pl.multiple_of(i * part_w, part_w), part_w)
+        return pltpu.make_async_copy(w_ref.at[span], w.at[span], in_sem.at[CHUNKS + i])
+
+    def hid_copy(i):
+        span = pl.ds(pl.multiple_of(i * part_w, part_w), part_w)
+        return pltpu.make_async_copy(hid_ref.at[:, span], hid.at[:, span], in_sem.at[i])
+
+    @pl.loop(0, CHUNKS)
+    def _(i):
+        w_copy(i).start()
+        hid_copy(i).start()
+
+
     barrier = pltpu.get_barrier_semaphore()
     for d in range(1, PLANE):
         pl.semaphore_signal(barrier, inc=1, device_id=plane_peer(d), device_id_type=MESH)
@@ -121,26 +142,7 @@
     def _(d):
         pl.semaphore_signal(barrier, inc=1, device_id=(c, d), device_id_type=MESH)
 
-    idx_copy = pltpu.make_async_copy(idx_ref, idx, in_sem.at[2 * CHUNKS])
-    idx_copy.start()
-
-    def w_copy(i):
-        span = pl.ds(pl.multiple_of(i * part_w, part_w), part_w)
-        return pltpu.make_async_copy(w_ref.at[span], w.at[span], in_sem.at[CHUNKS + i])
-
-    def hid_copy(i):
-        span = pl.ds(pl.multiple_of(i * part_w, part_w), part_w)
-        return pltpu.make_async_copy(hid_ref.at[:, span], hid.at[:, span], in_sem.at[i])
-
-    @pl.loop(0, CHUNKS)
-    def _(i):
-        w_copy(i).start()
-        hid_copy(i).start()
-
-    length_here = len_ref[0]
-    live = jnp.full((1, E), length_here, jnp.int32).astype(F32)
-
-    def count_step(i, total):
+    def count_step(length_here, i, total):
         span = pl.ds(pl.multiple_of(i * big, big), big)
         ids = lax.broadcasted_iota(jnp.int32, (E, big), 0).astype(BF16)
         named = idx[:, span].astype(F32)
@@ -182,8 +184,11 @@
     def plane_total(everyone, base):
         came(everyone.at[pl.ds(0, PLANE - 1)], st.at[base + 1])
         return jnp.sum(everyone[...], axis=0)
+    len_copy.wait()
     idx_copy.wait()
-    counts = lax.fori_loop(0, PARTS, count_step, jnp.zeros((8, E), F32))[:1]
+    length_here = len_ref[0]
+    live = jnp.full((1, E), length_here, jnp.int32).astype(F32)
+    counts = lax.fori_loop(0, PARTS, functools.partial(count_step, length_here), jnp.zeros((8, E), F32))[:1]
     pl.semaphore_wait(barrier, PLANE * (z + 1))
 
     @pl.loop(0, z)
@@ -218,12 +223,16 @@
         hid_copy(i).wait()
         sh[...] += jnp.dot(hid[:, span], w[span, :], preferred_element_type=F32)
 
-    pl.loop(0, CHUNKS)(logit_step)
+    pl.loop(0, CHUNKS - 1)(logit_step)
+    w_copy(CHUNKS - 1).wait()
+    hid_copy(CHUNKS - 1).wait()
+    last = pl.ds((CHUNKS - 1) * part_w, part_w)
 
     def score_step(i, total):
-        span = pl.ds(pl.multiple_of(i * big, big), big)
-        scores = jax.nn.sigmoid(sh[span, :])
-        at = me * tok + i * big + lax.broadcasted_iota(jnp.int32, (big, 1), 0)
+        span = pl.ds(i * small, small)
+        logits = sh[span, :] + jnp.dot(hid[span, last], w[last, :], preferred_element_type=F32)
+        scores = jax.nn.sigmoid(logits)
+        at = me * tok + i * small + lax.broadcasted_iota(jnp.int32, (small, 1), 0)
         valid = (at < length_here).astype(F32)
         share = scores / jnp.sum(scores, axis=1, keepdims=True)
         live_share = share * valid
@@ -231,7 +240,9 @@
         un[span, :] = live_share * (1.0 - scores)
         return total + jnp.sum(live_share, axis=0, keepdims=True)
 
-    score_local = lax.fori_loop(0, PARTS, score_step, jnp.zeros((1, E), F32))
+    score_local = jnp.zeros((1, E), F32)
+    for i in range(SMALL):
+        score_local = score_step(i, score_local)
     for k in range(LEVELS):
         @pl.when(z == k)
         def _():
@@ -313,13 +324,16 @@
         pair = pl.ds(pair_at(k, j), 2)
         s[pair] += acc[c, pair]
 
-        @pl.when((c == 0) & (k < 3))
+        @pl.when((c == 0) & (i < 7))
         def _():
             a_p(k, j).start()
 
-        @pl.when((c == 1) & (k < 3) & (j == 0))
+        @pl.when((c == 1) & (j == 0))
         def _():
             a_p(k, 0).start()
+
+        @pl.when((c == 1) & (j == 0) & (k < 3))
+        def _():
             a_p(k, 1).start()
 
         @pl.when(outer & (k < 3))
@@ -450,33 +464,32 @@
     b_pass(3, 1)
     b_pass(1, 1)
     a_turn(1, 1)
+    a_pass(0, 0)
+    a_turn(2, 0)
+    a_pass(0, 1)
+    a_join(1)
+    a_out(1)
     b_end()
     for o in range(2):
         b_p(o).start()
-    for o in range(2):
-        a_p(3, o).start()
-    a_pass(0, 0)
-    a_turn(2, 0)
-    a_join(1)
-    a_out(1)
-    a_pass(0, 1)
+    a_p(3, 1).start()
+    a_turn(2, 1)
+    a_pass(1, 0)
+    a_turn(3, 0)
+    a_pass(1, 1)
+    a_join(2)
+    a_out(2)
+    a_pass(3, 0)
+    a_pass(3, 1)
     b_turn(0)
-    a_turn(2, 1)
     b_turn(1)
     came(sco_z.at[pl.ds(0, LEVELS - 1)], st.at[7])
     mean_score = jnp.sum(sco_z[...], axis=0) / live
     bal_ref[...] = jnp.broadcast_to(jnp.sum(fraction * mean_score, axis=1, keepdims=True), bal_ref.shape)
-    a_pass(1, 0)
-    a_pass(1, 1)
-    a_turn(3, 0)
-    a_join(2)
-    a_out(2)
-    a_pass(3, 0)
-    a_pass(3, 1)
+    a_turn(3, 1)
     b_q.wait_recv()
     fin[c, hi] = s[z * 4 + here, hi] + rb3[2]
     fin_b.start()
-    a_turn(3, 1)
     a_join(3)
     a_end(0)
     a_end(1)
@@ -503,6 +516,16 @@
     sent(rbz.at[pl.ds(0, 3)], bz_s.at[0])
     sent(rb3, bp_s.at[0])
     sent(fin.at[c], f_s.at[0])
+
+
+def store(grad, bal, grad_out, bal_out, one, sem):
+    grad_copy = pltpu.make_async_copy(grad, grad_out, sem.at[0])
+    grad_copy.start()
+    one[0] = bal[0, 0]
+    bal_copy = pltpu.make_async_copy(one, bal_out, sem.at[1])
+    bal_copy.start()
+    grad_copy.wait()
+    bal_copy.wait()
 
 
 def fused(hidden, router_weight, expert_index, lengths):
@@ -521,11 +544,11 @@
             pl.BlockSpec(memory_space=pltpu.HBM),
             pl.BlockSpec(memory_space=pltpu.HBM),
             pl.BlockSpec(memory_space=pltpu.HBM),
-            pl.BlockSpec(memory_space=pltpu.SMEM),
+            pl.BlockSpec(memory_space=pltpu.HBM),
         ],
         out_specs=(pl.BlockSpec(memory_space=pltpu.VMEM), pl.BlockSpec(memory_space=pltpu.VMEM)),
         scratch_shapes=[
-            vm((TOPK, tok), jnp.int32), vm((tok, width), BF16), vm((width, E), BF16),
+            pltpu.SMEM((1,), jnp.int32), vm((TOPK, tok), jnp.int32), vm((tok, width), BF16), vm((width, E), BF16),
             vm((tok, E), F32), vm((tok, E), F32), vm((tok, 2 * E), BF16),
             vm((2, n, half, E), F32), vm((n, half, E), F32), vm((2, half, E), F32),
             vm((1, E), F32), vm((PLANE, 1, E), F32), vm((1, E), F32), vm((LEVELS, 1, E), F32),
@@ -533,7 +556,7 @@
             vm((1, E), F32), vm((PLANE, 1, E), F32), vm((1, E), F32), vm((LEVELS, 1, E), F32),
             vm((4, 2, qa, E), F32), vm((4, qa, E), F32), vm((2, 6, qa // 2, E), F32), vm((6, 2, 2, qb, E), F32),
             vm((3, qb, E), F32), pltpu.SemaphoreType.REGULAR,
-            dma((2 * CHUNKS + 1,)), dma((10,)), dma((1,)), dma((8,)),
+            dma((2 * CHUNKS + 2,)), dma((10,)), dma((1,)), dma((8,)),
             dma((1,)), dma((8,)), dma((1,)), dma((4,)), dma((1,)), dma((8,)), dma((1,)), dma((7,)),
             dma((1,)), dma((3,)), dma((1,)), dma((1,)),
         ],
@@ -541,7 +564,14 @@
             collective_id=0, has_side_effects=True, vmem_limit_bytes=62914560
         ),
     )(hidden, router_weight, expert_index.T, lengths)
-    return grad, bal[0, :1]
+    return pl.pallas_call(
+        store,
+        out_shape=(jax.ShapeDtypeStruct((block, E), F32), jax.ShapeDtypeStruct((1,), F32)),
+        in_specs=[pl.BlockSpec(memory_space=pltpu.VMEM), pl.BlockSpec(memory_space=pltpu.VMEM)],
+        out_specs=(pl.BlockSpec(memory_space=pltpu.HBM), pl.BlockSpec(memory_space=pltpu.HBM)),
+        scratch_shapes=[pltpu.SMEM((1,), F32), dma((2,))],
+        compiler_params=pltpu.CompilerParams(vmem_limit_bytes=1 << 20),
+    )(grad, bal)
 
 
 def solution(mesh):

time: 47.4 us -> 45.2 us (0.954)
  between operations: 2.45 us -> 1.28 us
  local copies, waits for them, and re-layouts: 0.77 us -> 0 us
    pallas_call x1, Pallas kernels: 44 us -> 43 us  [fused(): pl.pallas_call(functools.partial(kernel, n), out_shape=(pltpu.VMEM((block...]
    pallas_call x0 -> x1, Pallas kernels: none -> 0.8 us  [fused(): pl.pallas_call(store, out_shape=(jax.ShapeDtypeStruct((block, E), F32), j...]
    unnamed x1 -> x0, local copies, waits for them, and re-layouts: 0.77 us -> none
where the time goes in v3:
time: 45.2 us; the launch traced here: 45 us
  Pallas kernels  43.8 us (97%)
  between operations  1.28 us (3%)
    pallas_call x1, Pallas kernels, fused(): pl.pallas_call(functools.partial(kernel, n), out_shape=(pltpu.VMEM((block...  43 us

profile of v3, /device:TPU:0, one launch (start us, length us, event | category | flops | bytes accessed | tf_op | source)
XLA Modules:
  0.0 45.0 jit_solution(18291684068582704373)
XLA Ops:
  1.3 43.0 %shard_map.59 = (f32[448,256]{1,0:T(8,128)S(1)}, f32[1,128]{1,0:T(1,128)S(1)}) custom-call(bf16[1024,7168]{1,0:T(8,128)(2,1)} %hid_ref.1, bf16[7168,256]{1,0:T(8,128)(2,1)} %w_ref.1, s32[8,1024]{1,0:T(8,128)} %bitcast.1, s32[1]{0:T(128)S(6)} %copy.6.len_hbm), custom_call_target="tpu_custom_call" | custom-call | tf_op jit(solution)/shard_map/pallas_call | solution.py:540
  44.2 0.8 %shard_map.60 = (f32[448,256]{1,0:T(8,128)}, f32[1]{0:T(128)}) custom-call(f32[448,256]{1,0:T(8,128)S(1)} %get-tuple-element.4.grad, f32[1,128]{1,0:T(1,128)S(1)} %get-tuple-element.5.bal), custom_call_target="tpu_custom_call" | custom-call | tf_op jit(solution)/shard_map/pallas_call | solution.py:567

commit v4 on v3

--- a/solution.py
+++ b/solution.py
@@ -75,11 +75,11 @@
 
 
 def kernel(
-    n, hid_ref, w_ref, idx_ref, len_hbm, out_ref, bal_ref,
-    len_ref, idx, hid, w, sh, un, gcat, acc, s, fin,
+    n, hid_ref, w_ref, idx_ref, len_ref, out_ref, bal_ref,
+    idx, hid, w, sh, un, gcat, acc, s, fin,
     cnt, cnt_p, cnt_s, cnt_z, cnt_d, tot, sco, sco_p, sco_s, sco_z,
     ra1, ra2, raz, rbz, rb3,
-    up, in_sem, st, d_s, d_r, ap_s, ap_r, aq_s, aq_r, az_s, az_r, bz_s, bz_r, bp_s, bp_r, f_s, f_r,
+    up, in_sem, st, out_s, d_r, ap_r, aq_r, az_r, bz_r, bp_r, f_r,
 ):
     c = lax.axis_index("seq")
     me = lax.axis_index("ctx")
@@ -114,24 +114,28 @@
     qa = half - qb
     qh = qa // 2
 
-    len_copy = pltpu.make_async_copy(len_hbm, len_ref, in_sem.at[2 * CHUNKS + 1])
-    len_copy.start()
-    idx_copy = pltpu.make_async_copy(idx_ref, idx, in_sem.at[2 * CHUNKS])
+    idx_copy = pltpu.make_async_copy(idx_ref, idx, in_sem.at[CHUNKS])
     idx_copy.start()
 
     def w_copy(i):
         span = pl.ds(pl.multiple_of(i * part_w, part_w), part_w)
-        return pltpu.make_async_copy(w_ref.at[span], w.at[span], in_sem.at[CHUNKS + i])
+        return pltpu.make_async_copy(w_ref.at[span], w.at[span], in_sem.at[i])
 
     def hid_copy(i):
         span = pl.ds(pl.multiple_of(i * part_w, part_w), part_w)
         return pltpu.make_async_copy(hid_ref.at[:, span], hid.at[:, span], in_sem.at[i])
+
+    def loaded(i):
+        both = hid.at[:, pl.ds(0, part_w + part_w * E // tok)]
+        pltpu.make_async_copy(both, both, in_sem.at[i]).wait()
 
     @pl.loop(0, CHUNKS)
     def _(i):
         w_copy(i).start()
         hid_copy(i).start()
 
+    length_here = len_ref[0]
+    live = jnp.full((1, E), length_here, jnp.int32).astype(F32)
 
     barrier = pltpu.get_barrier_semaphore()
     for d in range(1, PLANE):
@@ -142,7 +146,7 @@
     def _(d):
         pl.semaphore_signal(barrier, inc=1, device_id=(c, d), device_id_type=MESH)
 
-    def count_step(length_here, i, total):
+    def count_step(i, total):
         span = pl.ds(pl.multiple_of(i * big, big), big)
         ids = lax.broadcasted_iota(jnp.int32, (E, big), 0).astype(BF16)
         named = idx[:, span].astype(F32)
@@ -184,11 +188,8 @@
     def plane_total(everyone, base):
         came(everyone.at[pl.ds(0, PLANE - 1)], st.at[base + 1])
         return jnp.sum(everyone[...], axis=0)
-    len_copy.wait()
     idx_copy.wait()
-    length_here = len_ref[0]
-    live = jnp.full((1, E), length_here, jnp.int32).astype(F32)
-    counts = lax.fori_loop(0, PARTS, functools.partial(count_step, length_here), jnp.zeros((8, E), F32))[:1]
+    counts = lax.fori_loop(0, PARTS, count_step, jnp.zeros((8, E), F32))[:1]
     pl.semaphore_wait(barrier, PLANE * (z + 1))
 
     @pl.loop(0, z)
@@ -219,13 +220,11 @@
                 up_copy(d).start()
 
         span = pl.ds(pl.multiple_of(i * part_w, part_w), part_w)
-        w_copy(i).wait()
-        hid_copy(i).wait()
+        loaded(i)
         sh[...] += jnp.dot(hid[:, span], w[span, :], preferred_element_type=F32)
 
     pl.loop(0, CHUNKS - 1)(logit_step)
-    w_copy(CHUNKS - 1).wait()
-    hid_copy(CHUNKS - 1).wait()
+    loaded(CHUNKS - 1)
     last = pl.ds((CHUNKS - 1) * part_w, part_w)
 
     def score_step(i, total):
@@ -281,7 +280,7 @@
 
     def pair_send(i):
         pair = pl.ds(pair_at(i // 2, i % 2), 2)
-        return remote(acc.at[1 - c, pair], s.at[pair], d_s.at[0], d_r.at[i], twin)
+        return remote(acc.at[1 - c, pair], s.at[pair], out_s.at[0], d_r.at[i], twin)
 
     lo, hi = pl.ds(0, qa), pl.ds(qa, qb)
 
@@ -291,11 +290,11 @@
     def a_p(k, o):
         zk = zs[k] if isinstance(k, int) else level(k)
         return remote(
-            s.at[zk * 4 + (1 - p) * sp + side(o) * sq, lo], ra1.at[k, o], ap_s.at[0], ap_r.at[2 * k + o], p_dev
+            s.at[zk * 4 + (1 - p) * sp + side(o) * sq, lo], ra1.at[k, o], out_s.at[0], ap_r.at[2 * k + o], p_dev
         )
 
     def a_q(k):
-        return remote(s.at[zs[k] * 4 + p * sp + (1 - q) * sq, lo], ra2.at[k], aq_s.at[0], aq_r.at[k], q_dev)
+        return remote(s.at[zs[k] * 4 + p * sp + (1 - q) * sq, lo], ra2.at[k], out_s.at[0], aq_r.at[k], q_dev)
 
     def a_at(k, h):
         return s.at[zs[k] * 4 + here, pl.ds(h * qh, qh)]
@@ -308,15 +307,15 @@
     AT = [0, 1, 3, 2, 4, 5]
 
     def a_z(i, h):
-        return remote(a_at(OF[i], h), raz.at[h, AT[i]], az_s.at[0], az_r.at[min(2 * AT[i], 6) + h], TO[i])
+        return remote(a_at(OF[i], h), raz.at[h, AT[i]], out_s.at[0], az_r.at[min(2 * AT[i], 6) + h], TO[i])
 
     def b_z(i, h):
-        return remote(b_at(OF[i], h), rbz.at[AT[i], h], bz_s.at[0], bz_r.at[2 * AT[i] + h if AT[i] < 3 else 6], TO[i])
+        return remote(b_at(OF[i], h), rbz.at[AT[i], h], out_s.at[0], bz_r.at[2 * AT[i] + h if AT[i] < 3 else 6], TO[i])
 
     def b_z_out(k, j):
         pair = pl.ds(pair_at(k, j), 2)
         slot = k + k // 2
-        return remote(s.at[pair, hi], rbz.at[slot, j], bz_s.at[0], bz_r.at[jnp.minimum(2 * slot + j, 6)], mate)
+        return remote(s.at[pair, hi], rbz.at[slot, j], out_s.at[0], bz_r.at[jnp.minimum(2 * slot + j, 6)], mate)
 
     def join(i):
         k, j = i // 2, i % 2
@@ -324,11 +323,13 @@
         pair = pl.ds(pair_at(k, j), 2)
         s[pair] += acc[c, pair]
 
-        @pl.when((c == 0) & (i < 7))
+        early = (k < 3) | (inner & (i == 6))
+
+        @pl.when((c == 0) & early)
         def _():
             a_p(k, j).start()
 
-        @pl.when((c == 1) & (j == 0))
+        @pl.when((c == 1) & (j == 0) & early)
         def _():
             a_p(k, 0).start()
 
@@ -389,9 +390,9 @@
                 b_at(3, h)[...] += rbz[3, h] + rbz[4, h]
 
     def b_p(o):
-        return remote(s.at[z * 4 + (1 - p) * sp + side(o) * sq, hi], rb3.at[o], bp_s.at[0], bp_r.at[o], p_dev)
-
-    b_q = remote(s.at[z * 4 + p * sp + (1 - q) * sq, hi], rb3.at[2], bp_s.at[0], bp_r.at[2], q_dev)
+        return remote(s.at[z * 4 + (1 - p) * sp + side(o) * sq, hi], rb3.at[o], out_s.at[0], bp_r.at[o], p_dev)
+
+    b_q = remote(s.at[z * 4 + p * sp + (1 - q) * sq, hi], rb3.at[2], out_s.at[0], bp_r.at[2], q_dev)
 
     def b_turn(o):
         b_p(o).wait_recv()
@@ -401,9 +402,9 @@
 
     def fin_a(h):
         part = fin.at[c, pl.ds(h * qh, qh)]
-        return remote(part, part, f_s.at[0], f_r.at[0], twin)
-
-    fin_b = remote(fin.at[c, hi], fin.at[c, hi], f_s.at[0], f_r.at[0], twin)
+        return remote(part, part, out_s.at[0], f_r.at[0], twin)
+
+    fin_b = remote(fin.at[c, hi], fin.at[c, hi], out_s.at[0], f_r.at[0], twin)
 
     def a_end(h):
         part = pl.ds(h * qh, qh)
@@ -464,25 +465,40 @@
     b_pass(3, 1)
     b_pass(1, 1)
     a_turn(1, 1)
+    a_turn(2, 0)
     a_pass(0, 0)
-    a_turn(2, 0)
     a_pass(0, 1)
     a_join(1)
     a_out(1)
+    @pl.when(outer)
+    def _():
+        a_p(3, 0).start()
     b_end()
     for o in range(2):
         b_p(o).start()
-    a_p(3, 1).start()
-    a_turn(2, 1)
-    a_pass(1, 0)
-    a_turn(3, 0)
-    a_pass(1, 1)
-    a_join(2)
-    a_out(2)
-    a_pass(3, 0)
-    a_pass(3, 1)
-    b_turn(0)
-    b_turn(1)
+
+    @pl.when(outer)
+    def _():
+        a_turn(2, 1)
+        a_p(3, 1).start()
+        a_join(2)
+        a_out(2)
+        a_turn(3, 0)
+        b_turn(0)
+        b_turn(1)
+
+    @pl.when(inner)
+    def _():
+        a_p(3, 1).start()
+        a_turn(2, 1)
+        a_pass(1, 0)
+        a_turn(3, 0)
+        a_pass(1, 1)
+        a_join(2)
+        a_pass(3, 0)
+        a_pass(3, 1)
+        b_turn(0)
+        b_turn(1)
     came(sco_z.at[pl.ds(0, LEVELS - 1)], st.at[7])
     mean_score = jnp.sum(sco_z[...], axis=0) / live
     bal_ref[...] = jnp.broadcast_to(jnp.sum(fraction * mean_score, axis=1, keepdims=True), bal_ref.shape)
@@ -509,22 +525,20 @@
             if k > 0:
                 sent(cnt_d.at[pl.ds(0, PLANE * k)], st.at[8])
 
-    sent(s, d_s.at[0])
-    sent(ra1, ap_s.at[0])
-    sent(ra2, aq_s.at[0])
-    sent(raz.at[0], az_s.at[0])
-    sent(rbz.at[pl.ds(0, 3)], bz_s.at[0])
-    sent(rb3, bp_s.at[0])
-    sent(fin.at[c], f_s.at[0])
+    sent(acc, out_s.at[0])
 
 
 def store(grad, bal, grad_out, bal_out, one, sem):
-    grad_copy = pltpu.make_async_copy(grad, grad_out, sem.at[0])
-    grad_copy.start()
+    rows = grad.shape[0] // 4
+    spans = [pl.ds(i * rows, rows) for i in range(4)]
+    copies = [pltpu.make_async_copy(grad.at[span], grad_out.at[span], sem.at[i]) for i, span in enumerate(spans)]
+    for copy in copies:
+        copy.start()
     one[0] = bal[0, 0]
-    bal_copy = pltpu.make_async_copy(one, bal_out, sem.at[1])
+    bal_copy = pltpu.make_async_copy(one, bal_out, sem.at[4])
     bal_copy.start()
-    grad_copy.wait()
+    for copy in copies:
+        copy.wait()
     bal_copy.wait()
 
 
@@ -544,11 +558,11 @@
             pl.BlockSpec(memory_space=pltpu.HBM),
             pl.BlockSpec(memory_space=pltpu.HBM),
             pl.BlockSpec(memory_space=pltpu.HBM),
-            pl.BlockSpec(memory_space=pltpu.HBM),
+            pl.BlockSpec(memory_space=pltpu.SMEM),
         ],
         out_specs=(pl.BlockSpec(memory_space=pltpu.VMEM), pl.BlockSpec(memory_space=pltpu.VMEM)),
         scratch_shapes=[
-            pltpu.SMEM((1,), jnp.int32), vm((TOPK, tok), jnp.int32), vm((tok, width), BF16), vm((width, E), BF16),
+            vm((TOPK, tok), jnp.int32), vm((tok, width), BF16), vm((width, E), BF16),
             vm((tok, E), F32), vm((tok, E), F32), vm((tok, 2 * E), BF16),
             vm((2, n, half, E), F32), vm((n, half, E), F32), vm((2, half, E), F32),
             vm((1, E), F32), vm((PLANE, 1, E), F32), vm((1, E), F32), vm((LEVELS, 1, E), F32),
@@ -556,9 +570,8 @@
             vm((1, E), F32), vm((PLANE, 1, E), F32), vm((1, E), F32), vm((LEVELS, 1, E), F32),
             vm((4, 2, qa, E), F32), vm((4, qa, E), F32), vm((2, 6, qa // 2, E), F32), vm((6, 2, 2, qb, E), F32),
             vm((3, qb, E), F32), pltpu.SemaphoreType.REGULAR,
-            dma((2 * CHUNKS + 2,)), dma((10,)), dma((1,)), dma((8,)),
-            dma((1,)), dma((8,)), dma((1,)), dma((4,)), dma((1,)), dma((8,)), dma((1,)), dma((7,)),
-            dma((1,)), dma((3,)), dma((1,)), dma((1,)),
+            dma((CHUNKS + 1,)), dma((10,)), dma((1,)), dma((8,)),
+            dma((8,)), dma((4,)), dma((8,)), dma((7,)), dma((3,)), dma((1,)),
         ],
         compiler_params=pltpu.CompilerParams(
             collective_id=0, has_side_effects=True, vmem_limit_bytes=62914560
@@ -569,7 +582,7 @@
         out_shape=(jax.ShapeDtypeStruct((block, E), F32), jax.ShapeDtypeStruct((1,), F32)),
         in_specs=[pl.BlockSpec(memory_space=pltpu.VMEM), pl.BlockSpec(memory_space=pltpu.VMEM)],
         out_specs=(pl.BlockSpec(memory_space=pltpu.HBM), pl.BlockSpec(memory_space=pltpu.HBM)),
-        scratch_shapes=[pltpu.SMEM((1,), F32), dma((2,))],
+        scratch_shapes=[pltpu.SMEM((1,), F32), dma((5,))],
         compiler_params=pltpu.CompilerParams(vmem_limit_bytes=1 << 20),
     )(grad, bal)
 

time: 45.2 us -> 45 us (level)
  no operation moved by 1% of the time
where the time goes in v4:
time: 45 us; the launch traced here: 44.9 us
  Pallas kernels  43.6 us (97%)
  between operations  1.28 us (3%)
    pallas_call x1, Pallas kernels, fused(): pl.pallas_call(functools.partial(kernel, n), out_shape=(pltpu.VMEM((block...  42.8 us

profile of v4, /device:TPU:0, one launch (start us, length us, event | category | flops | bytes accessed | tf_op | source)
XLA Modules:
  0.0 44.9 jit_solution(8919992826873776934)
XLA Ops:
  1.3 42.8 %shard_map.59 = (f32[448,256]{1,0:T(8,128)S(1)}, f32[1,128]{1,0:T(1,128)S(1)}) custom-call(bf16[1024,7168]{1,0:T(8,128)(2,1)} %hid_ref.1, bf16[7168,256]{1,0:T(8,128)(2,1)} %w_ref.1, s32[8,1024]{1,0:T(8,128)} %bitcast.1, s32[1]{0:T(128)S(6)} %copy.6.len_ref), custom_call_target="tpu_custom_call" | custom-call | tf_op jit(solution)/shard_map/pallas_call | solution.py:554
  44.0 0.8 %shard_map.60 = (f32[448,256]{1,0:T(8,128)}, f32[1]{0:T(128)}) custom-call(f32[448,256]{1,0:T(8,128)S(1)} %get-tuple-element.4.grad, f32[1,128]{1,0:T(1,128)S(1)} %get-tuple-element.5.bal), custom_call_target="tpu_custom_call" | custom-call | tf_op jit(solution)/shard_map/pallas_call | solution.py:580

commit v5 on v4

--- a/solution.py
+++ b/solution.py
@@ -470,9 +470,6 @@
     a_pass(0, 1)
     a_join(1)
     a_out(1)
-    @pl.when(outer)
-    def _():
-        a_p(3, 0).start()
     b_end()
     for o in range(2):
         b_p(o).start()
@@ -480,12 +477,13 @@
     @pl.when(outer)
     def _():
         a_turn(2, 1)
+        a_p(3, 0).start()
         a_p(3, 1).start()
         a_join(2)
         a_out(2)
-        a_turn(3, 0)
         b_turn(0)
         b_turn(1)
+        a_turn(3, 0)
 
     @pl.when(inner)
     def _():
@@ -502,10 +500,10 @@
     came(sco_z.at[pl.ds(0, LEVELS - 1)], st.at[7])
     mean_score = jnp.sum(sco_z[...], axis=0) / live
     bal_ref[...] = jnp.broadcast_to(jnp.sum(fraction * mean_score, axis=1, keepdims=True), bal_ref.shape)
-    a_turn(3, 1)
     b_q.wait_recv()
     fin[c, hi] = s[z * 4 + here, hi] + rb3[2]
     fin_b.start()
+    a_turn(3, 1)
     a_join(3)
     a_end(0)
     a_end(1)

time: 45 us -> 45.1 us (level)
  no operation moved by 1% of the time
where the time goes in v5:
time: 45.1 us; the launch traced here: 44.9 us
  Pallas kernels  43.7 us (97%)
  between operations  1.28 us (3%)
    pallas_call x1, Pallas kernels, fused(): pl.pallas_call(functools.partial(kernel, n), out_shape=(pltpu.VMEM((block...  42.8 us

profile of v5, /device:TPU:0, one launch (start us, length us, event | category | flops | bytes accessed | tf_op | source)
XLA Modules:
  0.0 44.9 jit_solution(16093392112931097701)
XLA Ops:
  1.3 42.8 %shard_map.59 = (f32[448,256]{1,0:T(8,128)S(1)}, f32[1,128]{1,0:T(1,128)S(1)}) custom-call(bf16[1024,7168]{1,0:T(8,128)(2,1)} %hid_ref.1, bf16[7168,256]{1,0:T(8,128)(2,1)} %w_ref.1, s32[8,1024]{1,0:T(8,128)} %bitcast.1, s32[1]{0:T(128)S(6)} %copy.6.len_ref), custom_call_target="tpu_custom_call" | custom-call | tf_op jit(solution)/shard_map/pallas_call | solution.py:552
  44.1 0.8 %shard_map.60 = (f32[448,256]{1,0:T(8,128)}, f32[1]{0:T(128)}) custom-call(f32[448,256]{1,0:T(8,128)S(1)} %get-tuple-element.4.grad, f32[1,128]{1,0:T(1,128)S(1)} %get-tuple-element.5.bal), custom_call_target="tpu_custom_call" | custom-call | tf_op jit(solution)/shard_map/pallas_call | solution.py:578
